TPU v7x, 32 devices: a whole 2x2x4 slice. The times are simulated.
32 devices in a mesh: groups: 2 (over y), cols: 4 (over z), rows: 4 (over x, core).
Axes of the slice: x: 2, y: 2, z: 4, core: 2. Of those that a mesh axis runs over, the one named last changes fastest.
Arguments:
- base_field: float32 [320, 64, 512], P(None, ('groups', 'cols'), 'rows'), parts along dimension 1, may hold values from -6 to 6
- control_field: float32 [320, 64, 512], P(None, ('groups', 'cols', 'rows')), parts along dimension 1, may hold values from -6 to 6
- first_kernel: bfloat16 [9, 320, 320], replicated, may hold values from -0.109375 to 0.109375
- second_kernel: bfloat16 [9, 320, 320], replicated, may hold values from -0.109375 to 0.109375
- control_kernel: bfloat16 [9, 320, 320], replicated, may hold values from -0.109375 to 0.109375
- first_bias: float32 [320], replicated, may hold values from -3 to 3
- second_bias: float32 [320], replicated, may hold values from -3 to 3
- control_bias: float32 [320], replicated, may hold values from -3 to 3
- to_control: bfloat16 [320, 320], replicated, may hold values from -0.3125 to 0.3125
- to_base: bfloat16 [320, 320], replicated, may hold values from -0.3125 to 0.3125
Outputs:
- base_out: float32 [320, 64, 512], P(None, ('groups', 'cols'), 'rows'), parts along dimension 1
- control_out: float32 [320, 64, 512], P(None, ('groups', 'cols', 'rows')), parts along dimension 1
There are 2 independent parts, one for each index of `groups`. A program takes and returns all parts, laid end to end along the dimension named above; an argument that names none is the same for every part. Nothing has to cross between parts.
All inputs are finite; a program needn't handle non-finite values.
Results may differ from a plain program's by a relative error of at most 0.0033.
Values may be sent and summed in bfloat16 or wider, within the bound.
A program may use at most 64 MiB of HBM per device.

v0:
```python
import jax
import jax.numpy as jnp
from jax import lax
from jax.sharding import PartitionSpec as P


def padded_2(value, sides, width):
    for axis, dim in sides:
        count, length = (lax.axis_size(axis), value.shape[dim])
        up = [(i, (i + 1) % count) for i in range(count - 1)]
        down = [(j, i) for i, j in up]
        last = lax.slice_in_dim(value, length - width, length, axis=dim)
        leading = lax.slice_in_dim(value, 0, width, axis=dim)
        before = lax.ppermute(last, axis, up)
        after = lax.ppermute(leading, axis, down)
        value = jnp.concatenate([before, value, after], axis=dim)
    return value


def convolve(padded, weight, bias):
    width = padded.shape[1] - 2
    height = padded.shape[2] - 2
    total = jnp.zeros((weight.shape[1], width, height), jnp.float32)
    for offset in range(9):
        across = offset // 3
        down = offset % 3
        window = padded[:, across : across + width, down : down + height]
        total = total + jnp.einsum(
            "oc,cwh->owh", weight[offset], window, preferred_element_type=jnp.float32
        )
    return total + bias[:, None, None]


def project(matrix, field):
    return jnp.einsum("oc,cwh->owh", matrix, field, preferred_element_type=jnp.float32)


def per_device(
    base_field,
    control_field,
    first_kernel,
    second_kernel,
    control_kernel,
    first_bias,
    second_bias,
    control_bias,
    to_control,
    to_base,
):
    base_round = base_field.astype(jnp.bfloat16)
    tile_cols = base_field.shape[1]
    tile_rows = base_field.shape[2]
    padded = padded_2(base_round, (("cols", 1), ("rows", 2)), 2)
    inner = jax.nn.silu(convolve(padded, first_kernel, first_bias))
    across = lax.axis_index("cols") * tile_cols - 1 + jnp.arange(tile_cols + 2, dtype=jnp.int32)
    downward = lax.axis_index("rows") * tile_rows - 1 + jnp.arange(tile_rows + 2, dtype=jnp.int32)
    col_inside = (across >= 0) & (across < tile_cols * lax.axis_size("cols"))
    row_inside = (downward >= 0) & (downward < tile_rows * lax.axis_size("rows"))
    inside = col_inside[:, None] & row_inside[None, :]
    hidden_ext = jnp.where(inside[None], inner, 0.0).astype(jnp.bfloat16)
    base_mid = jax.nn.silu(convolve(hidden_ext, second_kernel, second_bias)) + base_field
    base_send = base_mid.astype(jnp.bfloat16)
    control_round = control_field.astype(jnp.bfloat16)
    edged = padded_2(control_round, ((("cols", "rows"), 1),), 1)
    edged = jnp.pad(edged, ((0, 0), (0, 0), (1, 1)))
    control_mid = jax.nn.silu(convolve(edged, control_kernel, control_bias)) + control_field
    arrived = lax.all_to_all(base_send, "rows", split_axis=1, concat_axis=2, tiled=True)
    control_out = control_mid + project(to_control, arrived)
    control_send = control_out.astype(jnp.bfloat16)
    returned = lax.all_to_all(control_send, "rows", split_axis=2, concat_axis=1, tiled=True)
    base_out = base_mid + project(to_base, returned)
    return (base_out, control_out)


def solution(mesh):
    return jax.shard_map(
        per_device,
        mesh=mesh,
        in_specs=(
            P(None, ("groups", "cols"), "rows"),
            P(None, ("groups", "cols", "rows"), None),
            P(),
            P(),
            P(),
            P(),
            P(),
            P(),
            P(),
            P(),
        ),
        out_specs=(P(None, ("groups", "cols"), "rows"), P(None, ("groups", "cols", "rows"), None)),
        check_vma=False,
    )
```

profile of v0, /device:TPU:0, one launch (start us, length us, event | category | flops | bytes accessed | tf_op | source)
XLA Modules:
  0.0 80.0 jit_solution(4251604718525200333)
XLA Ops:
  0.7 1.8 %copy.29 = bf16[320,8,128]{0,2,1:T(8,128)(2,1)S(1)} copy(f32[320,8,128]{2,1,0:T(8,128)} %param.10) | data formatting | bytes 1966080 | tf_op args[0]
  2.5 0.8 fusion.120
  3.3 1.3 %collective-permute-start.1 = (bf16[320,2,128]{0,2,1:T(8,128)(2,1)}, bf16[320,2,128]{0,2,1:T(8,128)(2,1)S(1)}, u32[]{:S(2)}, u32[]{:S(2)}) collective-permute-start(bf16[320,2,128]{0,2,1:T(8,128)(2,1)} %get-tuple-element.9), channel_id=1, source_target_pairs={{4,0},{8,4},{12,8},{5,1},{9,5},{13,9},{6,2},{10,6},{14,10},{7,3},{... | collective-permute-start | bytes 491528 | tf_op jit(solution)/shard_map/ppermute | solution.py:15
  4.5 5.6 %collective-permute-start = (bf16[320,2,128]{0,2,1:T(8,128)(2,1)}, bf16[320,2,128]{0,2,1:T(8,128)(2,1)S(1)}, u32[]{:S(2)}, u32[]{:S(2)}) collective-permute-start(bf16[320,2,128]{0,2,1:T(8,128)(2,1)} %get-tuple-element.8), channel_id=1, source_target_pairs={{0,4},{4,8},{8,12},{1,5},{5,9},{9,13},{2,6},{6,10},{10,14},{3,7},{... | collective-permute-start | bytes 491528 | tf_op jit(solution)/shard_map/ppermute | solution.py:14
  10.4 0.9 %fusion.121 = (bf16[320,1,512]{2,0,1:T(8,128)(2,1)}, bf16[320,1,512]{2,0,1:T(8,128)(2,1)}) fusion(bf16[320,2,512]{2,0,1:T(8,128)(2,1)S(1)} %copy.64), kind=kLoop, calls=%fused_computation.151 | loop fusion | bytes 1310720 | tf_op jit(solution)/shard_map/slice | solution.py:12
  11.2 1.3 %collective-permute-start.5 = (bf16[320,1,512]{2,0,1:T(8,128)(2,1)}, bf16[320,1,512]{2,0,1:T(8,128)(2,1)}, u32[]{:S(2)}, u32[]{:S(2)}) collective-permute-start(bf16[320,1,512]{2,0,1:T(8,128)(2,1)} %get-tuple-element.11), channel_id=1, source_target_pairs={{1,0},{2,1},{3,2},{4,3},{5,4},{6,5},{7,6},{8,7},{9,8},{10,9},{11,1... | collective-permute-start | bytes 983048 | tf_op jit(solution)/shard_map/ppermute | solution.py:15
  12.5 3.8 %collective-permute-start.4 = (bf16[320,1,512]{2,0,1:T(8,128)(2,1)}, bf16[320,1,512]{2,0,1:T(8,128)(2,1)}, u32[]{:S(2)}, u32[]{:S(2)}) collective-permute-start(bf16[320,1,512]{2,0,1:T(8,128)(2,1)} %get-tuple-element.10), channel_id=1, source_target_pairs={{0,1},{1,2},{2,3},{3,4},{4,5},{5,6},{6,7},{7,8},{8,9},{9,10},{10,1... | collective-permute-start | bytes 983048 | tf_op jit(solution)/shard_map/ppermute | solution.py:14
  16.3 1.4 %fusion.59 = f32[320,2,512]{2,0,1:T(8,128)S(1)} fusion(bf16[320,2,512]{2,0,1:T(8,128)(2,1)S(1)} %copy.64, bf16[9,320,320]{2,1,0:T(8,128)(2,1)} %param.14), kind=kOutput, calls=%fused_computation.85 | convolution fusion | flops 209715200 | bytes 2211840 | tf_op jit(solution)/shard_map/oc,cwh->owh/dot_general | solution.py:28
  17.8 1.4 %collective-permute-start.3 = (bf16[320,12,2]{0,2,1:T(2,128)(2,1)S(1)}, bf16[320,12,2]{0,2,1:T(2,128)(2,1)S(1)}, u32[]{:S(2)}, u32[]{:S(2)}) collective-permute-start(bf16[320,12,2]{0,2,1:T(2,128)(2,1)S(1)} %get-tuple-element.7), channel_id=1, source_target_pairs={{1,0},{2,1},{3,2},{5,4},{6,5},{7,6},{9,8},{10,9},{11,10},{13,12},{... | collective-permute-start | bytes 46088 | tf_op jit(solution)/shard_map/ppermute | solution.py:15
  19.3 3.4 %collective-permute-start.2 = (bf16[320,12,2]{0,2,1:T(2,128)(2,1)S(1)}, bf16[320,12,2]{0,2,1:T(2,128)(2,1)S(1)}, u32[]{:S(2)}, u32[]{:S(2)}) collective-permute-start(bf16[320,12,2]{0,2,1:T(2,128)(2,1)S(1)} %get-tuple-element.6), channel_id=1, source_target_pairs={{0,1},{1,2},{2,3},{4,5},{5,6},{6,7},{8,9},{9,10},{10,11},{12,13},{... | collective-permute-start | bytes 46088 | tf_op jit(solution)/shard_map/ppermute | solution.py:14
  22.7 0.7 collective-permute-done.2
  24.0 0.8 %fusion.24 = f32[10,130,320]{2,1,0:T(8,128)S(1)} fusion(bf16[320,12,132]{0,2,1:T(8,128)(2,1)S(1)} %pad_maximum_fusion, bf16[9,320,320]{2,1,0:T(8,128)(2,1)S(1)} %copy-done.5), kind=kOutput, calls=%fused_computation.48 | convolution fusion | flops 266240000 | bytes 2954240 | tf_op jit(solution)/shard_map/oc,cwh->owh/dot_general | solution.py:28
  24.8 0.8 %fusion.26 = f32[10,130,320]{2,1,0:T(8,128)S(1)} fusion(bf16[320,12,132]{0,2,1:T(8,128)(2,1)S(1)} %pad_maximum_fusion, bf16[9,320,320]{2,1,0:T(8,128)(2,1)S(1)} %copy-done.5), kind=kOutput, calls=%fused_computation.50 | convolution fusion | flops 266240000 | bytes 2954240 | tf_op jit(solution)/shard_map/oc,cwh->owh/dot_general | solution.py:28
  25.6 0.8 %fusion.28 = f32[10,130,320]{2,1,0:T(8,128)S(1)} fusion(bf16[320,12,132]{0,2,1:T(8,128)(2,1)S(1)} %pad_maximum_fusion, bf16[9,320,320]{2,1,0:T(8,128)(2,1)S(1)} %copy-done.5), kind=kOutput, calls=%fused_computation.52 | convolution fusion | flops 266240000 | bytes 2954240 | tf_op jit(solution)/shard_map/oc,cwh->owh/dot_general | solution.py:28
  26.4 0.8 %fusion.79 = f32[10,130,320]{2,1,0:T(8,128)S(1)} fusion(bf16[9,320,320]{2,1,0:T(8,128)(2,1)S(1)} %copy-done.5, bf16[320,2,128]{0,2,1:T(8,128)(2,1)S(1)} %collective-permute-done.1, bf16[320,8,128]{0,2,1:T(8,128)(2,1)S(1)} %copy.29, bf16[320,2,128]{0,2,1:T(8,128)(2,1)S(1)} %collective-permute-done, bf16[320,12,2]{0,2,1:T(2,128)(2,1)S(1)} %collective-permute-done.2), kind=kOutput, calls=%fused_computation.103 | convolution fusion | flops 270233600 | bytes 3107840 | tf_op jit(solution)/shard_map/oc,cwh->owh/dot_general | solution.py:28
  27.2 0.8 fusion.81
  28.0 0.8 %fusion.84 = f32[10,130,320]{2,1,0:T(8,128)S(1)} fusion(bf16[9,320,320]{2,1,0:T(8,128)(2,1)S(1)} %copy-done.5, bf16[320,2,128]{0,2,1:T(8,128)(2,1)S(1)} %collective-permute-done.1, bf16[320,8,128]{0,2,1:T(8,128)(2,1)S(1)} %copy.29, bf16[320,2,128]{0,2,1:T(8,128)(2,1)S(1)} %collective-permute-done, bf16[320,12,2]{0,2,1:T(2,128)(2,1)S(1)} %collective-permute-done.2), kind=kOutput, calls=%fused_computation.108 | convolution fusion | flops 270233600 | bytes 3107840 | tf_op jit(solution)/shard_map/oc,cwh->owh/dot_general | solution.py:28
  28.8 0.8 fusion.86
  29.7 0.8 %fusion.89 = f32[10,130,320]{2,1,0:T(8,128)S(1)} fusion(bf16[9,320,320]{2,1,0:T(8,128)(2,1)S(1)} %copy-done.5, bf16[320,2,128]{0,2,1:T(8,128)(2,1)S(1)} %collective-permute-done.1, bf16[320,8,128]{0,2,1:T(8,128)(2,1)S(1)} %copy.29, bf16[320,2,128]{0,2,1:T(8,128)(2,1)S(1)} %collective-permute-done, bf16[320,12,2]{0,2,1:T(2,128)(2,1)S(1)} %collective-permute-done.2), kind=kOutput, calls=%fused_computation.113 | convolution fusion | flops 270233600 | bytes 3107840 | tf_op jit(solution)/shard_map/oc,cwh->owh/dot_general | solution.py:28
  30.5 2.3 %fusion.5 = bf16[320,10,130]{0,2,1:T(8,128)(2,1)S(1)} fusion(f32[10,130,320]{2,1,0:T(8,128)S(1)} %fusion.24, f32[10,130,320]{2,1,0:T(8,128)S(1)} %fusion.79, f32[10,130,320]{2,1,0:T(8,128)S(1)} %fusion.81, f32[10,130,320]{2,1,0:T(8,128)S(1)} %fusion.26, f32[10,130,320]{2,1,0:T(8,128)S(1)} %fusion.84, f32[10,130,320]{2,1,0:T(8,128)S(1)} %fusion.86, ...), kind=kOutput, calls=%fused_computation.9 | convolution fusion | flops 276473600 | bytes 18993664 | tf_op jit(solution)/shard_map/oc,cwh->owh/dot_general | solution.py:28
  32.9 0.5 fusion.38
  33.4 0.5 convolution_add_fusion.8
  33.9 0.5 convolution_add_fusion.7
  34.5 0.5 convolution_add_fusion.6
  35.0 0.5 convolution_add_fusion.5
  35.6 0.5 convolution_add_fusion.4
  36.2 0.5 convolution_add_fusion.3
  36.7 0.5 convolution_add_fusion.2
  37.3 0.7 copy-done.3
  38.0 1.7 %fusion.122 = (bf16[320,8,128]{2,0,1:T(8,128)(2,1)}, f32[320,8,128]{2,0,1:T(8,128)S(1)}) fusion(f32[320,8,128]{2,1,0:T(8,128)S(1)} %copy-done.3, f32[320]{0:T(512)S(1)} %copy-done.9, f32[8,128,320]{1,2,0:T(8,128)S(1)} %convolution_add_fusion.2, bf16[9,320,320]{2,1,0:T(8,128)(2,1)S(1)} %copy-done.2, bf16[320,10,130]{0,2,1:T(8,128)(2,1)S(1)} %fusion.5), kind=kOutput, calls=%fused_computation.152 | convolution fusion | flops 212336640 | bytes 5621760 | tf_op jit(solution)/shard_map/oc,cwh->owh/dot_general | solution.py:28
  39.8 5.2 %all-to-all-start = ((bf16[320,8,128]{2,0,1:T(8,128)(2,1)}), bf16[320,8,128]{2,0,1:T(8,128)(2,1)}, u32[]{:S(2)}, u32[]{:S(2)}) async-start(bf16[320,8,128]{2,0,1:T(8,128)(2,1)} %get-tuple-element.12), calls=%async_computation | async-start | bytes 1310720 | tf_op jit(solution)/shard_map/all_to_all | solution.py:67
  45.0 2.1 %fusion.10 = bf16[320,4,514]{2,0,1:T(8,128)(2,1)S(1)} fusion(bf16[320,1,512]{2,0,1:T(8,128)(2,1)} %collective-permute-done.5, bf16[320,2,512]{2,0,1:T(8,128)(2,1)S(1)} %copy.64, bf16[320,1,512]{2,0,1:T(8,128)(2,1)} %collective-permute-done.4), kind=kLoop, calls=%fused_computation.14 | loop fusion | flops 7895040 | bytes 2626560 | tf_op jit(solution)/shard_map/concatenate | solution.py:16
  47.1 0.6 convolution_bitcast_fusion.2
  47.7 0.5 convolution_bitcast_fusion.4
  48.2 0.6 convolution_bitcast_fusion.5
  48.9 0.5 fusion.46
  49.4 0.6 fusion.48
  50.0 1.5 %convolution_bitcast_fusion.3 = f32[320,2,512]{2,0,1:T(8,128)S(1)} fusion(bf16[320,1,512]{2,0,1:T(8,128)(2,1)} %collective-permute-done.5, bf16[320,2,512]{2,0,1:T(8,128)(2,1)S(1)} %copy.64, bf16[9,320,320]{2,1,0:T(8,128)(2,1)S(1)} %copy-done.1), kind=kOutput, calls=%fused_computation.38 | convolution fusion | flops 211025920 | bytes 2539520 | tf_op jit(solution)/shard_map/oc,cwh->owh/dot_general | solution.py:28
  51.5 1.5 %fusion.50 = f32[2,512,320]{1,2,0:T(8,128)S(1)} fusion(bf16[320,2,512]{2,0,1:T(8,128)(2,1)S(1)} %copy.64, bf16[320,1,512]{2,0,1:T(8,128)(2,1)} %collective-permute-done.4, bf16[9,320,320]{2,1,0:T(8,128)(2,1)S(1)} %copy-done.1), kind=kOutput, calls=%fused_computation.76 | convolution fusion | flops 211025920 | bytes 2539520 | tf_op jit(solution)/shard_map/oc,cwh->owh/dot_general | solution.py:28
  53.0 1.9 %fusion.23 = f32[320,2,512]{2,0,1:T(8,128)} fusion(f32[320,2,512]{2,0,1:T(8,128)S(1)} %convolution_bitcast_fusion.2, f32[320,2,512]{2,0,1:T(8,128)S(1)} %convolution_bitcast_fusion.3, f32[320,2,512]{2,0,1:T(8,128)S(1)} %convolution_bitcast_fusion.4, f32[320,2,512]{2,0,1:T(8,128)S(1)} %convolution_bitcast_fusion.5, f32[320,2,512]{2,0,1:T(8,128)S(1)} %fusion.59, ...), kind=kOutput, calls=%fused_computation.42 | convolution fusion | flops 212664320 | bytes 12699648 | tf_op jit(solution)/shard_map/oc,cwh->owh/dot_general | solution.py:28
  55.3 3.7 %fusion.123 = (bf16[320,2,512]{2,0,1:T(8,128)(2,1)S(1)}, f32[320,2,512]{2,0,1:T(8,128)}) fusion(bf16[4,2,40,8,128]{4,3,2,1,0:T(8,128)(2,1)} %bitcast.72, bf16[320,320]{1,0:T(8,128)(2,1)S(1)} %copy-done, f32[320,2,512]{2,1,0:T(2,128)} %param.11, f32[320,2,512]{2,0,1:T(8,128)} %fusion.23), kind=kOutput, calls=%fused_computation.153 | convolution fusion | flops 212008960 | bytes 5447680 | tf_op jit(solution)/shard_map/oc,cwh->owh/dot_general | solution.py:35
  59.0 1.9 %copy.43 = bf16[320,2,512]{0,1,2:T(2,128)(2,1)} copy(bf16[320,2,512]{2,0,1:T(8,128)(2,1)S(1)} %get-tuple-element.14) | data formatting | bytes 1310720 | tf_op jit(solution)/shard_map/convert_element_type | solution.py:69
  60.8 4.0 %all-to-all-start.1 = ((bf16[320,2,512]{0,1,2:T(2,128)(2,1)}), bf16[320,2,512]{0,1,2:T(2,128)(2,1)S(1)}, u32[]{:S(2)}, u32[]{:S(2)}) async-start(bf16[320,2,512]{0,1,2:T(2,128)(2,1)} %copy.43), calls=%async_computation.1 | async-start | bytes 1572864 | tf_op jit(solution)/shard_map/all_to_all | solution.py:70
  64.8 3.4 %copy.46 = f32[320,2,512]{2,1,0:T(2,128)} copy(f32[320,2,512]{2,0,1:T(8,128)} %get-tuple-element.15) | data formatting | bytes 2621440
  68.3 8.2 %all-to-all-done.1 = bf16[320,2,512]{0,1,2:T(2,128)(2,1)S(1)} async-done(((bf16[320,2,512]{0,1,2:T(2,128)(2,1)}), bf16[320,2,512]{0,1,2:T(2,128)(2,1)S(1)}, u32[]{:S(2)}, u32[]{:S(2)}) %all-to-all-start.1) | async-done | bytes 655392 | tf_op jit(solution)/shard_map/all_to_all | solution.py:70
  76.4 1.2 %copy.44 = bf16[320,2,4,128]{3,0,1,2:T(8,128)(2,1)S(1)} copy(bf16[320,2,4,128]{0,1,3,2:T(2,128)(2,1)S(1)} %bitcast.184) | data formatting | bytes 1310720 | tf_op jit(solution)/shard_map/all_to_all | solution.py:70
  77.6 0.5 fusion.20
  78.2 1.8 %copy.45 = f32[320,8,128]{2,1,0:T(8,128)} copy(f32[320,8,128]{2,0,1:T(8,128)S(1)} %fusion.20) | data formatting | bytes 2621440
  (31 shorter events, 1.3 us)
Async XLA Ops:
  0.6 54.7 %copy-start = (bf16[320,320]{1,0:T(8,128)(2,1)S(1)}, bf16[320,320]{1,0:T(8,128)(2,1)}, u32[]{:S(2)}) copy-start(bf16[320,320]{1,0:T(8,128)(2,1)} %param.18) | copy-start | bytes 614404
  0.6 9.5 %copy-start.4 = (f32[320,2,512]{2,1,0:T(2,128)S(1)}, f32[320,2,512]{2,1,0:T(2,128)}, u32[]{:S(2)}) copy-start(f32[320,2,512]{2,1,0:T(2,128)} %param.11) | copy-start | bytes 3932164
  3.3 14.5 %collective-permute-start.1 = (bf16[320,2,128]{0,2,1:T(8,128)(2,1)}, bf16[320,2,128]{0,2,1:T(8,128)(2,1)S(1)}, u32[]{:S(2)}, u32[]{:S(2)}) collective-permute-start(bf16[320,2,128]{0,2,1:T(8,128)(2,1)} %get-tuple-element.9), channel_id=1, source_target_pairs={{4,0},{8,4},{12,8},{5,1},{9,5},{13,9},{6,2},{10,6},{14,10},{7,3},{... | collective-permute-start | bytes 491528 | tf_op jit(solution)/shard_map/ppermute | solution.py:15
  4.5 13.2 %collective-permute-start = (bf16[320,2,128]{0,2,1:T(8,128)(2,1)}, bf16[320,2,128]{0,2,1:T(8,128)(2,1)S(1)}, u32[]{:S(2)}, u32[]{:S(2)}) collective-permute-start(bf16[320,2,128]{0,2,1:T(8,128)(2,1)} %get-tuple-element.8), channel_id=1, source_target_pairs={{0,4},{4,8},{8,12},{1,5},{5,9},{9,13},{2,6},{6,10},{10,14},{3,7},{... | collective-permute-start | bytes 491528 | tf_op jit(solution)/shard_map/ppermute | solution.py:14
  11.2 33.7 %collective-permute-start.5 = (bf16[320,1,512]{2,0,1:T(8,128)(2,1)}, bf16[320,1,512]{2,0,1:T(8,128)(2,1)}, u32[]{:S(2)}, u32[]{:S(2)}) collective-permute-start(bf16[320,1,512]{2,0,1:T(8,128)(2,1)} %get-tuple-element.11), channel_id=1, source_target_pairs={{1,0},{2,1},{3,2},{4,3},{5,4},{6,5},{7,6},{8,7},{9,8},{10,9},{11,1... | collective-permute-start | bytes 983048 | tf_op jit(solution)/shard_map/ppermute | solution.py:15
  12.5 32.5 %collective-permute-start.4 = (bf16[320,1,512]{2,0,1:T(8,128)(2,1)}, bf16[320,1,512]{2,0,1:T(8,128)(2,1)}, u32[]{:S(2)}, u32[]{:S(2)}) collective-permute-start(bf16[320,1,512]{2,0,1:T(8,128)(2,1)} %get-tuple-element.10), channel_id=1, source_target_pairs={{0,1},{1,2},{2,3},{3,4},{4,5},{5,6},{6,7},{7,8},{8,9},{9,10},{10,1... | collective-permute-start | bytes 983048 | tf_op jit(solution)/shard_map/ppermute | solution.py:14
  17.8 6.2 %copy-start.5 = (bf16[9,320,320]{2,1,0:T(8,128)(2,1)S(1)}, bf16[9,320,320]{2,1,0:T(8,128)(2,1)}, u32[]{:S(2)}) copy-start(bf16[9,320,320]{2,1,0:T(8,128)(2,1)} %param.12) | copy-start | bytes 5529604
  17.8 4.9 %collective-permute-start.3 = (bf16[320,12,2]{0,2,1:T(2,128)(2,1)S(1)}, bf16[320,12,2]{0,2,1:T(2,128)(2,1)S(1)}, u32[]{:S(2)}, u32[]{:S(2)}) collective-permute-start(bf16[320,12,2]{0,2,1:T(2,128)(2,1)S(1)} %get-tuple-element.7), channel_id=1, source_target_pairs={{1,0},{2,1},{3,2},{5,4},{6,5},{7,6},{9,8},{10,9},{11,10},{13,12},{... | collective-permute-start | bytes 46088 | tf_op jit(solution)/shard_map/ppermute | solution.py:15
  19.3 4.2 %collective-permute-start.2 = (bf16[320,12,2]{0,2,1:T(2,128)(2,1)S(1)}, bf16[320,12,2]{0,2,1:T(2,128)(2,1)S(1)}, u32[]{:S(2)}, u32[]{:S(2)}) collective-permute-start(bf16[320,12,2]{0,2,1:T(2,128)(2,1)S(1)} %get-tuple-element.6), channel_id=1, source_target_pairs={{0,1},{1,2},{2,3},{4,5},{5,6},{6,7},{8,9},{9,10},{10,11},{12,13},{... | collective-permute-start | bytes 46088 | tf_op jit(solution)/shard_map/ppermute | solution.py:14
  29.6 0.8 %copy-start.8 = (f32[320]{0:T(512)S(1)}, f32[320]{0:T(512)}, u32[]{:S(2)}) copy-start(f32[320]{0:T(512)} %param.15) | copy-start | bytes 3844
  30.5 2.4 %copy-start.2 = (bf16[9,320,320]{2,1,0:T(8,128)(2,1)S(1)}, bf16[9,320,320]{2,1,0:T(8,128)(2,1)}, u32[]{:S(2)}) copy-start(bf16[9,320,320]{2,1,0:T(8,128)(2,1)} %param.13) | copy-start | bytes 5529604
  36.7 1.3 %copy-start.3 = (f32[320,8,128]{2,1,0:T(8,128)S(1)}, f32[320,8,128]{2,1,0:T(8,128)}, u32[]{:S(2)}) copy-start(f32[320,8,128]{2,1,0:T(8,128)} %param.10) | copy-start | bytes 3932164
  36.7 1.3 %copy-start.9 = (f32[320]{0:T(512)S(1)}, f32[320]{0:T(512)}, u32[]{:S(2)}) copy-start(f32[320]{0:T(512)} %param.16) | copy-start | bytes 3844
  39.8 15.5 %all-to-all-start = ((bf16[320,8,128]{2,0,1:T(8,128)(2,1)}), bf16[320,8,128]{2,0,1:T(8,128)(2,1)}, u32[]{:S(2)}, u32[]{:S(2)}) async-start(bf16[320,8,128]{2,0,1:T(8,128)(2,1)} %get-tuple-element.12), calls=%async_computation | async-start | bytes 1310720 | tf_op jit(solution)/shard_map/all_to_all | solution.py:67
  45.0 2.1 %copy-start.1 = (bf16[9,320,320]{2,1,0:T(8,128)(2,1)S(1)}, bf16[9,320,320]{2,1,0:T(8,128)(2,1)}, u32[]{:S(2)}) copy-start(bf16[9,320,320]{2,1,0:T(8,128)(2,1)} %param.14) | copy-start | bytes 5529604
  51.5 1.5 %copy-start.7 = (f32[320]{0:T(512)S(1)}, f32[320]{0:T(512)}, u32[]{:S(2)}) copy-start(f32[320]{0:T(512)} %param.17) | copy-start | bytes 3844
  60.8 15.6 %all-to-all-start.1 = ((bf16[320,2,512]{0,1,2:T(2,128)(2,1)}), bf16[320,2,512]{0,1,2:T(2,128)(2,1)S(1)}, u32[]{:S(2)}, u32[]{:S(2)}) async-start(bf16[320,2,512]{0,1,2:T(2,128)(2,1)} %copy.43), calls=%async_computation.1 | async-start | bytes 1572864 | tf_op jit(solution)/shard_map/all_to_all | solution.py:70
  64.8 12.8 %copy-start.6 = (bf16[320,320]{1,0:T(8,128)(2,1)S(1)}, bf16[320,320]{1,0:T(8,128)(2,1)}, u32[]{:S(2)}) copy-start(bf16[320,320]{1,0:T(8,128)(2,1)} %param.19) | copy-start | bytes 614404
where the time goes:
time: 80.5 us; the launch traced here: 80 us
  matrix products  28.2 us (35%)
  starting transfers between devices  25.9 us (32%)
  local copies, waits for them, and re-layouts  12.8 us (16%)
  waiting for transfers between devices  9.34 us (12%)
  other arithmetic  2.73 us (3%)
  between operations  1.07 us (1%)
    dot_general x27, matrix products, convolve(): jnp.einsum('oc,cwh->owh', weight[offset], window, preferred_element_type=...  24 us
    ppermute x3, starting transfers between devices, padded_2(): before = lax.ppermute(last, axis, up)  12.7 us
    all_to_all x1, waiting for transfers between devices, per_device(): lax.all_to_all(control_send, 'rows', split_axis=2, concat_axis=1, tiled=T...  8.19 us
    unnamed x24, local copies, waits for them, and re-layouts  8.05 us
    all_to_all x1, starting transfers between devices, per_device(): lax.all_to_all(base_send, 'rows', split_axis=1, concat_axis=2, tiled=True)  5.23 us
    dot_general x2, matrix products, project(): jnp.einsum('oc,cwh->owh', matrix, field, preferred_element_type=jnp.float32)  4.17 us
    all_to_all x1, starting transfers between devices, per_device(): lax.all_to_all(control_send, 'rows', split_axis=2, concat_axis=1, tiled=T...  3.99 us
    ppermute x3, starting transfers between devices, padded_2(): after = lax.ppermute(leading, axis, down)  3.98 us
  transfers between devices with their start and end apart: 8, of which 3 were waited for; matrix products, arithmetic and copies ran while one was open for 39% of the time, Pallas kernels for 0%

commit v1 on v0

v1 whole, which is shorter than its diff:
```python
import functools

import jax
import jax.numpy as jnp
from jax import lax
from jax.experimental import pallas as pl
from jax.experimental.pallas import tpu as pltpu
from jax.sharding import PartitionSpec as P

MESH = pl.DeviceIdType.MESH
BF = jnp.bfloat16
F32 = jnp.float32
LANE = 128
PACK = 16
SIDES = ((-1, 0), (1, 0), (0, -1), (0, 1), (-1, -1), (1, -1), (-1, 1), (1, 1))


def silu(v):
    return 0.5 * v * (1.0 + jnp.tanh(0.5 * v))


def kernel(
    n_cols,
    n_rows,
    base_hbm,
    control_hbm,
    k1_hbm,
    k2_hbm,
    kc_hbm,
    b1_ref,
    b2_ref,
    bc_ref,
    tc_ref,
    tb_ref,
    base_out,
    control_out,
    base,
    control,
    raw,
    packed,
    shifts_b,
    shifts_h,
    shifts_c,
    biases,
    edge_out,
    edge_in,
    strips,
    mid,
    result,
    bracket,
    arrived,
    load_sem,
    x_send,
    x_recv,
    in_send,
    in_recv,
    out_send,
    out_recv,
):
    C = base.shape[0]
    tile_cols = base.shape[1]
    strip_cols = control.shape[1]
    wide = strip_cols * LANE
    main = C - C % LANE
    rest = C - main
    full = packed.shape[1] - C
    gid = lax.axis_index("groups")
    k = lax.axis_index("cols")
    r = lax.axis_index("rows")
    lane = lax.broadcasted_iota(jnp.int32, (C, LANE), 1)

    loads = []
    for i, (src, dst) in enumerate(
        (
            (base_hbm, base),
            (control_hbm, control),
            (k1_hbm, raw.at[0]),
            (k2_hbm, raw.at[1]),
            (kc_hbm, raw.at[2]),
        )
    ):
        copy = pltpu.make_async_copy(src, dst, load_sem.at[i])
        copy.start()
        loads.append(copy)

    def there(side):
        dk, dr = side
        ok = None
        for at, step, count in ((k, dk, n_cols), (r, dr, n_rows)):
            if step:
                test = (at > 0) if step < 0 else (at < count - 1)
                ok = test if ok is None else jnp.logical_and(ok, test)
        return ok

    def partner(o):
        if n_rows & (n_rows - 1):
            return lax.rem(r + o, n_rows), lax.rem(r + n_rows - o, n_rows)
        q, bit = r, 1
        while bit < n_rows:
            if o & bit:
                q = q + bit * (1 - 2 * lax.rem(lax.div(r, bit), 2))
            bit *= 2
        return q, q

    order = [o for o in range(n_rows // 2, n_rows)] + [o for o in range(1, n_rows // 2)]

    barrier = pltpu.get_barrier_semaphore()
    peers = n_rows - 1
    for side in SIDES:
        if side[0]:
            peers = peers + jnp.where(there(side), 1, 0)

            @pl.when(there(side))
            def _():
                pl.semaphore_signal(
                    barrier, inc=1, device_id=(gid, k + side[0], r + side[1]), device_id_type=MESH
                )
    for o in order:
        pl.semaphore_signal(barrier, inc=1, device_id=(gid, k, partner(o)[0]), device_id_type=MESH)

    def entered():
        pl.semaphore_wait(barrier, peers)

    def slot(s, count=1):
        return pl.ds(s * LANE, count * LANE)

    blocks = {(0, -1): 0, (-1, -1): 1, (1, -1): 2, (0, 1): 3, (-1, 1): 4, (1, 1): 5}

    def exchange(index, shifts):
        made = []
        for i, side in enumerate(SIDES):
            dk, dr = side
            if dr == 0:
                src = shifts.at[1, :, slot(1 if dk < 0 else tile_cols)]
                dst = shifts.at[1, :, slot(tile_cols + 1 if dk < 0 else 0)]
            else:
                src = edge_out.at[index, pl.ds(0 if dr < 0 else PACK, PACK), :]
                dst = edge_in.at[index, pl.ds(PACK * blocks[(-dk, -dr)], PACK), :]
            made.append(
                pltpu.make_async_remote_copy(
                    src_ref=src,
                    dst_ref=dst,
                    send_sem=x_send.at[index, i],
                    recv_sem=x_recv.at[index, i],
                    device_id=(gid, k + dk, r + dr),
                    device_id_type=MESH,
                )
            )
        return made

    def opposite(i):
        return SIDES.index((-SIDES[i][0], -SIDES[i][1]))

    def send_edges(index, shifts):
        made = exchange(index, shifts)
        for i in (3, 2, 0, 1, 4, 5, 6, 7):
            @pl.when(there(SIDES[i]))
            def _():
                made[i].start()

    def await_edges(index, shifts):
        made = exchange(index, shifts)
        for i, side in enumerate(SIDES):
            @pl.when(there(side))
            def _():
                made[opposite(i)].wait_recv()

    def await_sent(index, shifts):
        made = exchange(index, shifts)
        for i, side in enumerate(SIDES):
            @pl.when(there(side))
            def _():
                made[i].wait_send()

    def clear_edges(index, shifts):
        for side in SIDES:
            dk, dr = side

            @pl.when(jnp.logical_not(there(side)))
            def _():
                if dr == 0:
                    shifts[1, :, slot(0 if dk < 0 else tile_cols + 1)] = jnp.zeros((C, LANE), BF)
                else:
                    edge_in[index, pl.ds(PACK * blocks[side], PACK), :] = jnp.zeros(
                        (PACK, edge_in.shape[2]), BF
                    )

    def pack_column(edges, w, value):
        edges = jnp.where(lane == w + 1, value[:, 0:1], edges)
        return jnp.where(lane == PACK + w + 1, value[:, LANE - 1 : LANE], edges)

    def store_edges(index, edges):
        spare = edge_out.shape[2] - C
        tall = jnp.concatenate([edges, jnp.zeros((spare, LANE), F32)], axis=0)
        edge_out[index] = tall.T[: 2 * PACK].astype(BF)

    def make_shifts(index, shifts):
        halo = edge_in[index].astype(F32).T[:C]
        for s in range(tile_cols + 2):
            if s == 0:
                at = PACK + tile_cols
            elif s == tile_cols + 1:
                at = 2 * PACK + 1
            else:
                at = s
            value = shifts[1, :, slot(s)].astype(F32)
            before = jnp.where(lane == 0, halo[:, at : at + 1], pltpu.roll(value, 1, 1))
            at += 3 * PACK
            after = jnp.where(
                lane == LANE - 1, halo[:, at : at + 1], pltpu.roll(value, LANE - 1, 1)
            )
            shifts[0, :, slot(s)] = before.astype(BF)
            shifts[2, :, slot(s)] = after.astype(BF)

    def pack_weights(i):
        loads[2 + i].wait()
        for t in range(9):
            packed[i, :, pl.ds(t * main, main)] = raw[i, t, :, :main]
        for t in range(0, 9, 2):
            here = raw[i, t, :, main:]
            at = 9 * main + t * rest
            if t < 8:
                here = jnp.concatenate([here, raw[i, t + 1, :, main:]], axis=1)
            packed[i, :, pl.ds(at, here.shape[1])] = here

    def convolve(i, shifts, q):
        pieces, last = [], []
        for t in range(9):
            at = pl.ds(pl.multiple_of((q * strip_cols + t // 3) * LANE, LANE), wide)
            pieces.append(shifts[t % 3, :main, at])
            last.append(shifts[t % 3, main:, at])
        patch = jnp.concatenate(pieces + last, axis=0)
        total = jnp.dot(packed[i], patch, preferred_element_type=F32)
        return total + jnp.concatenate([biases[i]] * strip_cols, axis=1)

    def part(q):
        return pl.ds(pl.multiple_of(q * wide, LANE), wide)

    def inner(q):
        return pl.ds(pl.multiple_of(q * wide + LANE, LANE), wide)

    loads[0].wait()
    edges = jnp.zeros((C, LANE), F32)
    for w in range(tile_cols):
        value = base[:, w, :].astype(BF)
        shifts_b[1, :, slot(w + 1)] = value
        edges = pack_column(edges, w, value.astype(F32))
    store_edges(0, edges)
    entered()
    send_edges(0, shifts_b)

    loads[1].wait()
    for q in range(n_rows):
        strips[q] = jnp.concatenate(
            [control[:, w, pl.ds(q * LANE, LANE)] for w in range(strip_cols)], axis=1
        ).astype(BF)

    def to_tile(j, o):
        q, _ = partner(o)
        return pltpu.make_async_remote_copy(
            src_ref=strips.at[q],
            dst_ref=shifts_c.at[1, :, inner(r)],
            send_sem=in_send.at[j],
            recv_sem=in_recv.at[j],
            device_id=(gid, k, q),
            device_id_type=MESH,
        )

    def to_strip(j, o):
        q, _ = partner(o)
        return pltpu.make_async_remote_copy(
            src_ref=bracket.at[q],
            dst_ref=arrived.at[r],
            send_sem=out_send.at[j],
            recv_sem=out_recv.at[j],
            device_id=(gid, k, q),
            device_id_type=MESH,
        )

    for j, o in enumerate(order):
        to_tile(j, o).start()
    shifts_c[1, :, inner(r)] = strips[r]

    for i, (index, ref) in enumerate(((0, b1_ref), (1, b2_ref), (2, bc_ref))):
        row = jnp.concatenate([ref[...], jnp.zeros((1, edge_out.shape[2] - C), F32)], axis=1)
        biases[i] = jnp.broadcast_to(row, (LANE, edge_out.shape[2])).T[:C]
    for index, shifts in enumerate((shifts_b, shifts_h, shifts_c)):
        clear_edges(index, shifts)
    pack_weights(0)

    await_edges(0, shifts_b)
    make_shifts(0, shifts_b)
    edges = jnp.zeros((C, LANE), F32)
    for q in range(n_rows):
        value = silu(convolve(0, shifts_b, q)).astype(BF)
        shifts_h[1, :, pl.ds(q * wide + LANE, wide)] = value
        for w in range(strip_cols):
            edges = pack_column(
                edges, q * strip_cols + w, value[:, w * LANE : (w + 1) * LANE].astype(F32)
            )
    store_edges(1, edges)
    send_edges(1, shifts_h)
    pack_weights(1)
    pack_weights(2)

    for j, o in enumerate(order):
        to_tile(j, o).wait_recv()
    edges = jnp.zeros((C, LANE), F32)
    for w in range(tile_cols):
        edges = pack_column(edges, w, shifts_c[1, :, slot(w + 1)].astype(F32))
    store_edges(2, edges)
    send_edges(2, shifts_c)

    await_edges(1, shifts_h)
    make_shifts(1, shifts_h)
    for q in range(n_rows):
        own = jnp.concatenate([base[:, q * strip_cols + w, :] for w in range(strip_cols)], axis=1)
        mid[:, pl.ds(q * wide, wide)] = silu(convolve(1, shifts_h, q)) + own

    await_edges(2, shifts_c)
    make_shifts(2, shifts_c)
    for j, o in enumerate(order + [0]):
        q = partner(o)[0] if o else r
        here = mid[:, part(q)]
        change = silu(convolve(2, shifts_c, q)) + jnp.dot(
            tc_ref[...], here.astype(BF), preferred_element_type=F32
        )
        bracket[q] = change.astype(BF)
        if o:
            to_strip(j, o).start()
        send = (change + shifts_c[1, :, inner(q)].astype(F32)).astype(BF)
        result[:, part(q)] = here + jnp.dot(tb_ref[...], send, preferred_element_type=F32)
    arrived[r] = bracket[r]

    for w in range(tile_cols):
        base_out[:, w, :] = result[:, slot(w)]
    for j, o in enumerate(order):
        to_strip(j, o).wait_recv()
    for q in range(n_rows):
        for w in range(strip_cols):
            at = pl.ds(q * LANE, LANE)
            control_out[:, w, at] = control[:, w, at] + arrived[q, :, slot(w)].astype(F32)
    for index, shifts in enumerate((shifts_b, shifts_h, shifts_c)):
        await_sent(index, shifts)
    for j, o in enumerate(order):
        to_tile(j, o).wait_send()
        to_strip(j, o).wait_send()


def solution(mesh):
    n_cols, n_rows = mesh.shape["cols"], mesh.shape["rows"]

    def per_device(base, control, k1, k2, kc, b1, b2, bc, tc, tb):
        C, tile_cols, _ = base.shape
        strip_cols = control.shape[1]
        wide = strip_cols * LANE
        tall = -(-C // LANE) * LANE
        area = tile_cols * LANE
        held = pltpu.VMEM((3, C, area + 2 * LANE), BF)
        others = n_rows - 1
        any_spec = pl.BlockSpec(memory_space=pl.ANY)
        vmem = pl.BlockSpec(memory_space=pltpu.VMEM)
        return pl.pallas_call(
            functools.partial(kernel, n_cols, n_rows),
            out_shape=(
                jax.ShapeDtypeStruct(base.shape, F32),
                jax.ShapeDtypeStruct(control.shape, F32),
            ),
            in_specs=[any_spec] * 5 + [vmem] * 5,
            out_specs=(vmem, vmem),
            scratch_shapes=[
                pltpu.VMEM(base.shape, F32),
                pltpu.VMEM(control.shape, F32),
                pltpu.VMEM((3,) + k1.shape, BF),
                pltpu.VMEM((3, C, 9 * C), BF),
                held,
                held,
                held,
                pltpu.VMEM((3, C, LANE), F32),
                pltpu.VMEM((3, 2 * PACK, tall), BF),
                pltpu.VMEM((3, LANE, tall), BF),
                pltpu.VMEM((n_rows, C, wide), BF),
                pltpu.VMEM((C, area), F32),
                pltpu.VMEM((C, area), F32),
                pltpu.VMEM((n_rows, C, wide), BF),
                pltpu.VMEM((n_rows, C, wide), BF),
                pltpu.SemaphoreType.DMA((5,)),
                pltpu.SemaphoreType.DMA((3, 8)),
                pltpu.SemaphoreType.DMA((3, 8)),
                pltpu.SemaphoreType.DMA((others,)),
                pltpu.SemaphoreType.DMA((others,)),
                pltpu.SemaphoreType.DMA((others,)),
                pltpu.SemaphoreType.DMA((others,)),
            ],
            compiler_params=pltpu.CompilerParams(
                collective_id=0, has_side_effects=True, vmem_limit_bytes=60 * 1024 * 1024
            ),
        )(base, control, k1, k2, kc, b1[None], b2[None], bc[None], tc, tb)

    tiles = P(None, ("groups", "cols"), "rows")
    lines = P(None, ("groups", "cols", "rows"), None)
    return jax.shard_map(
        per_device,
        mesh=mesh,
        in_specs=(tiles, lines) + (P(),) * 8,
        out_specs=(tiles, lines),
        check_vma=False,
    )
```

time: 80.5 us -> 46.7 us (0.58)
  Pallas kernels: 0 us -> 38.1 us
  matrix products: 28.2 us -> 0 us
  starting transfers between devices: 25.9 us -> 0 us
  waiting for transfers between devices: 9.34 us -> 0 us
  local copies, waits for them, and re-layouts: 12.8 us -> 7.38 us
  other arithmetic: 2.73 us -> 0 us
    pallas_call x0 -> x1, Pallas kernels: none -> 38.1 us  [per_device(): pl.pallas_call(functools.partial(kernel, n_cols, n_rows), out_shape=(jax....]
    dot_general x29 -> x0, matrix products: 28.2 us -> none  [the longest x27 24 us: convolve(): jnp.einsum('oc,cwh->owh', weight[offset], window, preferred_element_type=...]
    ppermute x6 -> x0, starting transfers between devices: 16.7 us -> none  [the longest x3 12.7 us: padded_2(): before = lax.ppermute(last, axis, up)]
    all_to_all x2 -> x0, starting transfers between devices: 9.21 us -> none  [the longest x1 5.23 us: per_device(): lax.all_to_all(base_send, 'rows', split_axis=1, concat_axis=2, tiled=True)]
    all_to_all x2 -> x0, waiting for transfers between devices: 8.58 us -> none  [the longest x1 8.19 us: per_device(): lax.all_to_all(control_send, 'rows', split_axis=2, concat_axis=1, tiled=T...]
    unnamed x24 -> x4, local copies, waits for them, and re-layouts: 8.05 us -> 3.62 us
    broadcast_in_dim x0 -> x3, local copies, waits for them, and re-layouts: none -> 3.76 us  [the longest x1 1.27 us: per_device(): bc[None]]
    concatenate x2 -> x0, other arithmetic: 2.6 us -> none  [padded_2(): value = jnp.concatenate([before, value, after], axis=dim)]
  transfers between devices with their start and end apart: 8 -> 0, of which waited for: 3 -> 0; matrix products, arithmetic and copies ran while one was open for 39% -> 0% of each run, Pallas kernels for 0% -> 0%
where the time goes in v1:
time: 46.7 us; the launch traced here: 46.2 us
  Pallas kernels  38.1 us (82%)
  local copies, waits for them, and re-layouts  7.38 us (16%)
  between operations  0.65 us (1%)
    pallas_call x1, Pallas kernels, per_device(): pl.pallas_call(functools.partial(kernel, n_cols, n_rows), out_shape=(jax....  38.1 us
    unnamed x4, local copies, waits for them, and re-layouts  3.62 us
    broadcast_in_dim x1, local copies, waits for them, and re-layouts, per_device(): bc[None]  1.27 us
    broadcast_in_dim x1, local copies, waits for them, and re-layouts, per_device(): b1[None]  1.25 us
    broadcast_in_dim x1, local copies, waits for them, and re-layouts, per_device(): b2[None]  1.24 us

profile of v1, /device:TPU:0, one launch (start us, length us, event | category | flops | bytes accessed | tf_op | source)
XLA Modules:
  0.0 46.2 jit_solution(11115016459466685277)
XLA Ops:
  0.6 1.2 %broadcast_in_dim.9.b1_ref = f32[1,320]{1,0:T(1,128)} reshape(f32[320]{0:T(512)} %param.15) | data formatting | bytes 2560 | tf_op jit(solution)/shard_map/broadcast_in_dim | solution.py:398
  1.9 1.2 %broadcast_in_dim.10.b2_ref = f32[1,320]{1,0:T(1,128)} reshape(f32[320]{0:T(512)} %param.16) | data formatting | bytes 2560 | tf_op jit(solution)/shard_map/broadcast_in_dim | solution.py:398
  3.1 1.3 %broadcast_in_dim.11.bc_ref = f32[1,320]{1,0:T(1,128)} reshape(f32[320]{0:T(512)} %param.17) | data formatting | bytes 2560 | tf_op jit(solution)/shard_map/broadcast_in_dim | solution.py:398
  4.4 38.1 %shard_map.113 = (f32[320,8,128]{2,1,0:T(8,128)}, f32[320,2,512]{2,1,0:T(2,128)}) custom-call(f32[320,8,128]{2,1,0:T(8,128)} %base_hbm.1, f32[320,2,512]{2,1,0:T(2,128)} %control_hbm.1, bf16[9,320,320]{2,1,0:T(8,128)(2,1)} %k1_hbm.1, bf16[9,320,320]{2,1,0:T(8,128)(2,1)} %k2_hbm.1, bf16[9,320,320]{2,1,0:T(8,128)(2,1)} %kc_hbm.1, ...), custom_call_target="tpu_custom_call" | custom-call | tf_op jit(solution)/shard_map/pallas_call | solution.py:363
  42.5 0.0 copy-start
  42.6 2.6 %copy.14 = f32[320,8,128]{2,1,0:T(8,128)} copy(f32[320,8,128]{2,1,0:T(8,128)} %get-tuple-element.4) | data formatting | bytes 2621440
  45.1 0.0 copy-done
  45.1 1.1 %copy.15 = f32[320,2,512]{2,1,0:T(2,128)} copy(f32[320,2,512]{2,1,0:T(2,128)S(1)} %copy-done) | data formatting | bytes 2621440
Async XLA Ops:
  42.5 2.6 %copy-start = (f32[320,2,512]{2,1,0:T(2,128)S(1)}, f32[320,2,512]{2,1,0:T(2,128)}, u32[]{:S(2)}) copy-start(f32[320,2,512]{2,1,0:T(2,128)} %get-tuple-element.5) | copy-start | bytes 3932164
